TPU v7x, 32 devices: a whole 2x2x4 slice. The times are simulated.
32 devices in a mesh: row: 4 (over y, core), col: 8 (over z, x).
Axes of the slice: x: 2, y: 2, z: 4, core: 2. Of those that a mesh axis runs over, the one named last changes fastest.
Arguments:
- residuals: bfloat16 [16384, 32], P(('row', 'col')), may hold values from -6 to 6
- intersect_blocks: int32 [32, 4], P(('row', 'col')), may hold values from 0 to 3
- local_inverse: bfloat16 [16384, 1024], P(('row', 'col')), may hold values from -0.1875 to 0.1875
- coarse_basis: float32 [32768, 64], P(('row', 'col')), may hold values from -0.1875 to 0.1875
- coarse_slots: int32 [2048], replicated, may hold values from 0 to 2047, each once
- coarse_inverse: float32 [2048, 2048], P('row', 'col'), may hold values from -0.5 to 0.5
Outputs:
- preconditioned: float32 [16384, 32], P(('row', 'col'))
Inputs may be any that keep to these rules, and one draw needn't show every extreme that they name: `intersect_blocks`: each entry names one of the four owned blocks. `coarse_slots`: every coarse index from 0 to 2047 appears exactly once.
All inputs are finite; a program needn't handle non-finite values.
Results may differ from a plain program's by a relative error of at most 0.0003.
Values may be sent and summed in bfloat16 or wider, within the bound.
A program may use at most 64 MiB of HBM per device.

v0:
```python
import jax
import jax.numpy as jnp
from jax import lax
from jax.sharding import PartitionSpec as P

BLK = 128


def extended(cells, sides, width, closed):
    for axis, dim in sides:
        count = lax.axis_size(axis)
        ends = count if closed else count - 1
        head = lax.slice_in_dim(cells, 0, width, axis=dim)
        tail = lax.slice_in_dim(cells, cells.shape[dim] - width, cells.shape[dim], axis=dim)
        cells = jnp.concatenate(
            [
                lax.ppermute(tail, axis, [(i, (i + 1) % count) for i in range(ends)]),
                cells,
                lax.ppermute(head, axis, [((i + 1) % count, i) for i in range(ends)]),
            ],
            axis=dim,
        )
    return cells


def shards(residuals, intersect_blocks, local_inverse, coarse_basis, coarse_slots, coarse_inverse):
    own_rows = residuals.shape[0]
    rhs_count = residuals.shape[1]
    nev_count = coarse_basis.shape[1]
    blocks = residuals.reshape(own_rows // BLK, BLK, rhs_count)
    send_index = intersect_blocks[0]
    outgoing = jnp.take(blocks, send_index, axis=0)
    padded = extended(outgoing[None, None], (("row", 0), ("col", 1)), 1, False)
    incoming = jnp.stack([padded[0, 1, 0], padded[2, 1, 1], padded[1, 0, 2], padded[1, 2, 3]])
    local_vec = jnp.concatenate([residuals, incoming.reshape(-1, rhs_count)], axis=0)
    schwarz = jnp.dot(local_inverse, local_vec, preferred_element_type=jnp.float32)
    partial_sums = jnp.dot(
        coarse_basis.T, local_vec.astype(jnp.float32), precision=lax.Precision.HIGHEST
    )
    column_width = coarse_inverse.shape[1]
    col_offset = lax.axis_index("col") * column_width

    def add_piece(carry, piece):
        shifted = lax.slice_in_dim(coarse_slots, 0, piece.shape[0], axis=0) - col_offset
        inside = (shifted >= 0) & (shifted < column_width)
        target = jnp.where(inside, shifted, column_width)
        return carry.at[target].add(piece, mode="drop")

    column_part = add_piece(
        jnp.zeros((column_width, rhs_count), jnp.float32),
        jax.tree.map(lambda a: lax.all_gather(a, ("row", "col"), axis=0, tiled=True), partial_sums),
    )
    product = jnp.dot(coarse_inverse, column_part, precision=lax.Precision.HIGHEST)
    row_total = lax.psum(product, "col")
    whole_coarse = lax.all_gather(row_total, "row", axis=0, tiled=True)
    my_slots = lax.dynamic_slice_in_dim(
        coarse_slots, lax.axis_index(("row", "col")) * nev_count, nev_count, 0
    )
    own_coarse = jnp.take(whole_coarse, my_slots, axis=0)
    prolonged = jnp.dot(coarse_basis, own_coarse, precision=lax.Precision.HIGHEST)
    returning = prolonged[own_rows:].reshape(-1, BLK, rhs_count)
    padded_back = extended(returning[None, None], (("row", 0), ("col", 1)), 1, False)
    returned = jnp.stack(
        [padded_back[2, 1, 0], padded_back[0, 1, 1], padded_back[1, 2, 2], padded_back[1, 0, 3]]
    )
    matches = (send_index[:, None] == jnp.arange(own_rows // BLK, dtype=jnp.int32)[None, :]).astype(
        jnp.float32
    )
    added = jnp.einsum("db,dkr->bkr", matches, returned, precision=lax.Precision.HIGHEST)
    return schwarz + prolonged[:own_rows] + added.reshape(own_rows, rhs_count)


def solution(mesh):
    placed = (
        P(("row", "col"), None),
        P(("row", "col"), None),
        P(("row", "col"), None),
        P(("row", "col"), None),
        P(),
        P("row", "col"),
    )
    return jax.shard_map(
        shards, mesh=mesh, in_specs=placed, out_specs=P(("row", "col"), None), check_vma=False
    )
```

profile of v0, /device:TPU:0, one launch (start us, length us, event | category | flops | bytes accessed | tf_op | source)
XLA Modules:
  0.0 212.3 jit_solution(17657866889500280651)
XLA Ops:
  6.5 0.8 fusion.18
  7.3 0.8 copy_bitcast_fusion
  8.1 0.6 gather_fusion
  8.8 2.4 %collective-permute-start = (bf16[1,1,4,128,32]{3,4,2,1,0:T(8,128)(2,1)S(1)}, bf16[1,1,4,128,32]{3,4,2,1,0:T(8,128)(2,1)S(1)}, u32[]{:S(2)}, u32[]{:S(2)}) collective-permute-start(bf16[1,1,4,128,32]{3,4,2,1,0:T(8,128)(2,1)S(1)} %bitcast_select_fusion), channel_id=1, source_target_pairs={{0,8},{8,16},{16,24},{1,9},{9,17},{17,25},{2,10},{10,18},{18,26},{... | collective-permute-start | bytes 98312 | tf_op jit(solution)/shard_map/ppermute | solution.py:17
  11.2 1.3 collective-permute-start.1
  12.6 3.8 %collective-permute-done.1 = bf16[1,1,4,128,32]{3,4,2,1,0:T(8,128)(2,1)S(1)} collective-permute-done((bf16[1,1,4,128,32]{3,4,2,1,0:T(8,128)(2,1)S(1)}, bf16[1,1,4,128,32]{3,4,2,1,0:T(8,128)(2,1)S(1)}, u32[]{:S(2)}, u32[]{:S(2)}) %collective-permute-start.1) | collective-permute-done | bytes 32800 | tf_op jit(solution)/shard_map/ppermute | solution.py:19
  16.4 1.3 collective-permute-start.3
  17.7 4.6 %collective-permute-start.2 = (bf16[3,1,4,128,32]{3,4,2,1,0:T(8,128)(2,1)S(1)}, bf16[3,1,4,128,32]{3,4,2,1,0:T(8,128)(2,1)S(1)}, u32[]{:S(2)}, u32[]{:S(2)}) collective-permute-start(bf16[3,1,4,128,32]{3,4,2,1,0:T(8,128)(2,1)S(1)} %pad_maximum_fusion), channel_id=1, source_target_pairs={{0,1},{1,2},{2,3},{3,4},{4,5},{5,6},{6,7},{8,9},{9,10},{10,11},{11... | collective-permute-start | bytes 294920 | tf_op jit(solution)/shard_map/ppermute | solution.py:17
  22.3 0.6 collective-permute-done.3
  22.9 3.2 %collective-permute-done.2 = bf16[3,1,4,128,32]{3,4,2,1,0:T(8,128)(2,1)S(1)} collective-permute-done((bf16[3,1,4,128,32]{3,4,2,1,0:T(8,128)(2,1)S(1)}, bf16[3,1,4,128,32]{3,4,2,1,0:T(8,128)(2,1)S(1)}, u32[]{:S(2)}, u32[]{:S(2)}) %collective-permute-start.2) | collective-permute-done | bytes 98336 | tf_op jit(solution)/shard_map/ppermute | solution.py:17
  26.4 68.6 %all-gather = f32[32,64,32]{1,2,0:T(8,128)S(1)} all-gather(f32[1,64,32]{1,2,0:T(8,128)S(1)} %convolution_bitcast_fusion.3), channel_id=1, replica_groups=mesh['row'=4,'col'=8] {'row','col'}, dimensions={0}, use_global_device_ids=true | all-gather | bytes 270336 | tf_op jit(solution)/shard_map/all_gather | solution.py:51
  95.4 11.5 %scatter_custom_fusion = f32[256,32]{1,0:T(8,128)S(1)} fusion(s32[2048]{0:T(1024)S(1)} %compare_select_fusion, f32[2048,32]{1,0:T(8,128)S(1)} %bitcast.68, f32[]{:T(128)} %constant.48.clone.1), kind=kCustom, calls=%fused_computation.18 | custom fusion | flops 65536 | bytes 32772 | tf_op jit(solution)/shard_map/scatter-add | solution.py:47
  106.9 1.3 convolution_bitcast_fusion.1
  108.2 68.8 %all-reduce.2.cloned.1.call-done = f32[512,32]{0,1:T(8,128)} async-done(((f32[512,32]{0,1:T(8,128)}), f32[512,32]{0,1:T(8,128)}) %all-reduce.2.cloned.1.call-update) | async-done | bytes 65552 | tf_op jit(solution)/shard_map/psum | solution.py:54
  177.0 6.0 %all_gather.7 = f32[2048,32]{0,1:T(8,128)S(1)} all-gather(f32[512,32]{0,1:T(8,128)} %all-reduce.2.cloned.1.call-done), channel_id=1, replica_groups=mesh['row'=4,'col'=8] {'row'}, dimensions={0}, use_global_device_ids=true | all-gather | bytes 327680 | tf_op jit(solution)/shard_map/all_gather | solution.py:55
  183.3 0.6 gather_fusion.1
  184.3 2.3 %collective-permute-start.5 = (f32[1,1,4,128,32]{3,4,2,1,0:T(8,128)S(1)}, f32[1,1,4,128,32]{3,4,2,1,0:T(8,128)S(1)}, u32[]{:S(2)}, u32[]{:S(2)}) collective-permute-start(f32[1,1,4,128,32]{3,4,2,1,0:T(8,128)S(1)} %copy.40), channel_id=1, source_target_pairs={{0,8},{8,16},{16,24},{1,9},{9,17},{17,25},{2,10},{10,18},{18,26},{... | collective-permute-start | bytes 196616 | tf_op jit(solution)/shard_map/ppermute | solution.py:17
  186.6 1.3 collective-permute-start.4
  187.9 2.5 %collective-permute-done.4 = f32[1,1,4,128,32]{3,4,2,1,0:T(8,128)S(1)} collective-permute-done((f32[1,1,4,128,32]{3,4,2,1,0:T(8,128)S(1)}, f32[1,1,4,128,32]{3,4,2,1,0:T(8,128)S(1)}, u32[]{:S(2)}, u32[]{:S(2)}) %collective-permute-start.4) | collective-permute-done | bytes 65568 | tf_op jit(solution)/shard_map/ppermute | solution.py:19
  190.5 1.3 collective-permute-start.6
  191.8 4.6 %collective-permute-start.7 = (f32[3,1,4,128,32]{3,4,2,1,0:T(8,128)S(1)}, f32[3,1,4,128,32]{3,4,2,1,0:T(8,128)S(1)}, u32[]{:S(2)}, u32[]{:S(2)}) collective-permute-start(f32[3,1,4,128,32]{3,4,2,1,0:T(8,128)S(1)} %constant_dynamic-update-slice_fusion.1), channel_id=1, source_target_pairs={{0,1},{1,2},{2,3},{3,4},{4,5},{5,6},{6,7},{8,9},{9,10},{10,11},{11... | collective-permute-start | bytes 589832 | tf_op jit(solution)/shard_map/ppermute | solution.py:17
  196.4 1.8 collective-permute-done.6
  198.2 6.0 %collective-permute-done.7 = f32[3,1,4,128,32]{3,4,2,1,0:T(8,128)S(1)} collective-permute-done((f32[3,1,4,128,32]{3,4,2,1,0:T(8,128)S(1)}, f32[3,1,4,128,32]{3,4,2,1,0:T(8,128)S(1)}, u32[]{:S(2)}, u32[]{:S(2)}) %collective-permute-start.7) | collective-permute-done | bytes 196640 | tf_op jit(solution)/shard_map/ppermute | solution.py:17
  204.4 1.1 fusion.1
  (50 shorter events, 1.9 us)
Async XLA Ops:
  6.5 197.9 %copy-start = (bf16[512,1024]{1,0:T(8,128)(2,1)S(1)}, bf16[512,1024]{1,0:T(8,128)(2,1)}, u32[]{:S(2)}) copy-start(bf16[512,1024]{1,0:T(8,128)(2,1)} %param.8) | copy-start | bytes 3145732
  6.5 0.8 copy-start.7
  6.5 170.4 %all-reduce.2.cloned.1.call-start = ((), (), s32[]{:S(2)}) async-start(), calls=%async_computation | async-start | bytes 131072 | tf_op jit(solution)/shard_map/psum | solution.py:54
  8.1 4.4 %copy-start.3 = (bf16[512,32]{0,1:T(8,128)(2,1)S(1)}, bf16[512,32]{0,1:T(8,128)(2,1)}, u32[]{:S(2)}) copy-start(bf16[512,32]{0,1:T(8,128)(2,1)} %param.6) | copy-start | bytes 98308
  8.1 4.4 %copy-start.6 = (s32[2048]{0:T(1024)S(1)}, s32[2048]{0:T(1024)}, u32[]{:S(2)}) copy-start(s32[2048]{0:T(1024)} %param.10) | copy-start | bytes 24580
  8.7 17.5 %copy-start.1 = (f32[1024,64]{0,1:T(8,128)S(1)}, f32[1024,64]{0,1:T(8,128)}, u32[]{:S(2)}) copy-start(f32[1024,64]{0,1:T(8,128)} %param.9) | copy-start | bytes 786436
  8.8 3.8 %collective-permute-start = (bf16[1,1,4,128,32]{3,4,2,1,0:T(8,128)(2,1)S(1)}, bf16[1,1,4,128,32]{3,4,2,1,0:T(8,128)(2,1)S(1)}, u32[]{:S(2)}, u32[]{:S(2)}) collective-permute-start(bf16[1,1,4,128,32]{3,4,2,1,0:T(8,128)(2,1)S(1)} %bitcast_select_fusion), channel_id=1, source_target_pairs={{0,8},{8,16},{16,24},{1,9},{9,17},{17,25},{2,10},{10,18},{18,26},{... | collective-permute-start | bytes 98312 | tf_op jit(solution)/shard_map/ppermute | solution.py:17
  11.2 5.2 %collective-permute-start.1 = (bf16[1,1,4,128,32]{3,4,2,1,0:T(8,128)(2,1)S(1)}, bf16[1,1,4,128,32]{3,4,2,1,0:T(8,128)(2,1)S(1)}, u32[]{:S(2)}, u32[]{:S(2)}) collective-permute-start(bf16[1,1,4,128,32]{3,4,2,1,0:T(8,128)(2,1)S(1)} %bitcast_select_fusion), channel_id=1, source_target_pairs={{8,0},{16,8},{24,16},{9,1},{17,9},{25,17},{10,2},{18,10},{26,18},{... | collective-permute-start | bytes 98312 | tf_op jit(solution)/shard_map/ppermute | solution.py:19
  16.4 6.5 %collective-permute-start.3 = (bf16[3,1,4,128,32]{3,4,2,1,0:T(8,128)(2,1)S(1)}, bf16[3,1,4,128,32]{3,4,2,1,0:T(8,128)(2,1)S(1)}, u32[]{:S(2)}, u32[]{:S(2)}) collective-permute-start(bf16[3,1,4,128,32]{3,4,2,1,0:T(8,128)(2,1)S(1)} %pad_maximum_fusion), channel_id=1, source_target_pairs={{1,0},{2,1},{3,2},{4,3},{5,4},{6,5},{7,6},{9,8},{10,9},{11,10},{12... | collective-permute-start | bytes 294920 | tf_op jit(solution)/shard_map/ppermute | solution.py:19
  17.7 8.4 %collective-permute-start.2 = (bf16[3,1,4,128,32]{3,4,2,1,0:T(8,128)(2,1)S(1)}, bf16[3,1,4,128,32]{3,4,2,1,0:T(8,128)(2,1)S(1)}, u32[]{:S(2)}, u32[]{:S(2)}) collective-permute-start(bf16[3,1,4,128,32]{3,4,2,1,0:T(8,128)(2,1)S(1)} %pad_maximum_fusion), channel_id=1, source_target_pairs={{0,1},{1,2},{2,3},{3,4},{4,5},{5,6},{6,7},{8,9},{9,10},{10,11},{11... | collective-permute-start | bytes 294920 | tf_op jit(solution)/shard_map/ppermute | solution.py:17
  95.0 11.9 %copy-start.2 = (f32[512,256]{1,0:T(8,128)S(1)}, f32[512,256]{1,0:T(8,128)}, u32[]{:S(2)}) copy-start(f32[512,256]{1,0:T(8,128)} %param.11) | copy-start | bytes 1572868
  184.3 3.6 %collective-permute-start.5 = (f32[1,1,4,128,32]{3,4,2,1,0:T(8,128)S(1)}, f32[1,1,4,128,32]{3,4,2,1,0:T(8,128)S(1)}, u32[]{:S(2)}, u32[]{:S(2)}) collective-permute-start(f32[1,1,4,128,32]{3,4,2,1,0:T(8,128)S(1)} %copy.40), channel_id=1, source_target_pairs={{0,8},{8,16},{16,24},{1,9},{9,17},{17,25},{2,10},{10,18},{18,26},{... | collective-permute-start | bytes 196616 | tf_op jit(solution)/shard_map/ppermute | solution.py:17
  186.6 3.9 %collective-permute-start.4 = (f32[1,1,4,128,32]{3,4,2,1,0:T(8,128)S(1)}, f32[1,1,4,128,32]{3,4,2,1,0:T(8,128)S(1)}, u32[]{:S(2)}, u32[]{:S(2)}) collective-permute-start(f32[1,1,4,128,32]{3,4,2,1,0:T(8,128)S(1)} %copy.40), channel_id=1, source_target_pairs={{8,0},{16,8},{24,16},{9,1},{17,9},{25,17},{10,2},{18,10},{26,18},{... | collective-permute-start | bytes 196616 | tf_op jit(solution)/shard_map/ppermute | solution.py:19
  187.9 8.5 %copy-start.4 = (f32[1,1,4,128,32]{3,4,2,1,0:T(8,128)}, f32[1,1,4,128,32]{3,4,2,1,0:T(8,128)S(1)}, u32[]{:S(2)}) copy-start(f32[1,1,4,128,32]{3,4,2,1,0:T(8,128)S(1)} %collective-permute-done.5) | copy-start | bytes 196612
  190.5 5.9 %copy-start.5 = (f32[1,1,4,128,32]{3,4,2,1,0:T(8,128)}, f32[1,1,4,128,32]{3,4,2,1,0:T(8,128)S(1)}, u32[]{:S(2)}) copy-start(f32[1,1,4,128,32]{3,4,2,1,0:T(8,128)S(1)} %collective-permute-done.4) | copy-start | bytes 196612
  190.5 7.7 %collective-permute-start.6 = (f32[3,1,4,128,32]{3,4,2,1,0:T(8,128)S(1)}, f32[3,1,4,128,32]{3,4,2,1,0:T(8,128)S(1)}, u32[]{:S(2)}, u32[]{:S(2)}) collective-permute-start(f32[3,1,4,128,32]{3,4,2,1,0:T(8,128)S(1)} %constant_dynamic-update-slice_fusion.1), channel_id=1, source_target_pairs={{1,0},{2,1},{3,2},{4,3},{5,4},{6,5},{7,6},{9,8},{10,9},{11,10},{12... | collective-permute-start | bytes 589832 | tf_op jit(solution)/shard_map/ppermute | solution.py:19
  191.8 12.4 %collective-permute-start.7 = (f32[3,1,4,128,32]{3,4,2,1,0:T(8,128)S(1)}, f32[3,1,4,128,32]{3,4,2,1,0:T(8,128)S(1)}, u32[]{:S(2)}, u32[]{:S(2)}) collective-permute-start(f32[3,1,4,128,32]{3,4,2,1,0:T(8,128)S(1)} %constant_dynamic-update-slice_fusion.1), channel_id=1, source_target_pairs={{0,1},{1,2},{2,3},{3,4},{4,5},{5,6},{6,7},{8,9},{9,10},{10,11},{11... | collective-permute-start | bytes 589832 | tf_op jit(solution)/shard_map/ppermute | solution.py:17
  198.2 6.0 %slice-start = ((f32[1,1,4,128,32]{3,4,2,1,0:T(8,128)}), f32[1,1,1,128,32]{3,4,2,1,0:T(8,128)S(1)}, s32[]{:S(2)}) async-start(f32[1,1,4,128,32]{3,4,2,1,0:T(8,128)} %copy-done.4), calls=%async_computation.1 | async-start | bytes 32768 | tf_op jit(solution)/shard_map/slice | solution.py:64
  198.2 6.0 %slice-start.1 = ((f32[1,1,4,128,32]{3,4,2,1,0:T(8,128)}), f32[1,1,1,128,32]{3,4,2,1,0:T(8,128)S(1)}, s32[]{:S(2)}) async-start(f32[1,1,4,128,32]{3,4,2,1,0:T(8,128)} %copy-done.5), calls=%async_computation.2 | async-start | bytes 32768 | tf_op jit(solution)/shard_map/slice | solution.py:64
Sparse Core Ops, SparseCore 0:
  108.3 68.6 all-reduce.1
where the time goes:
time: 213 us; the launch traced here: 212 us
  waiting for transfers between devices  86.8 us (41%)
  blocking collectives  74.5 us (35%)
  starting transfers between devices  18.9 us (9%)
  between operations  13.7 us (6%)
  other arithmetic  12.5 us (6%)
  matrix products  3.19 us (1%)
  local copies, waits for them, and re-layouts  2.73 us (1%)
    psum x1, waiting for transfers between devices, shards(): row_total = lax.psum(product, 'col')  68.8 us
    all_gather x1, blocking collectives, shards(): lax.all_gather(a, ('row', 'col'), axis=0, tiled=True)  68.6 us
    ppermute x4, starting transfers between devices, extended(): lax.ppermute(tail, axis, [(i, (i + 1) % count) for i in range(ends)])  13.8 us
    scatter-add x1, other arithmetic, add_piece(): return carry.at[target].add(piece, mode='drop')  11.5 us
    ppermute x4, waiting for transfers between devices, extended(): lax.ppermute(tail, axis, [(i, (i + 1) % count) for i in range(ends)])  9.19 us
    ppermute x4, waiting for transfers between devices, extended(): lax.ppermute(head, axis, [((i + 1) % count, i) for i in range(ends)])  8.76 us
    all_gather x1, blocking collectives, shards(): whole_coarse = lax.all_gather(row_total, 'row', axis=0, tiled=True)  5.97 us
    ppermute x4, starting transfers between devices, extended(): lax.ppermute(head, axis, [((i + 1) % count, i) for i in range(ends)])  5.17 us
  transfers between devices with their start and end apart: 9, of which 7 were waited for; matrix products, arithmetic and copies ran while one was open for 0% of the time, Pallas kernels for 0%

commit v1 on v0

--- a/solution.py
+++ b/solution.py
@@ -51,7 +51,7 @@
         jax.tree.map(lambda a: lax.all_gather(a, ("row", "col"), axis=0, tiled=True), partial_sums),
     )
     product = jnp.dot(coarse_inverse, column_part, precision=lax.Precision.HIGHEST)
-    row_total = lax.psum(product, "col")
+    row_total = jnp.sum(lax.all_gather(product, "col"), axis=0)
     whole_coarse = lax.all_gather(row_total, "row", axis=0, tiled=True)
     my_slots = lax.dynamic_slice_in_dim(
         coarse_slots, lax.axis_index(("row", "col")) * nev_count, nev_count, 0

time: 213 us -> 164 us (0.77)
  waiting for transfers between devices: 86.8 us -> 13.5 us
  blocking collectives: 74.5 us -> 112 us
  between operations: 13.7 us -> 0.32 us
    psum x1 -> x0, waiting for transfers between devices: 68.8 us -> none  [shards(): row_total = lax.psum(product, 'col')]
    all_gather x0 -> x1, blocking collectives: none -> 31.6 us  [shards(): row_total = jnp.sum(lax.all_gather(product, 'col'), axis=0)]
    all_gather x1, blocking collectives: 5.97 us -> 11.7 us  [shards(): whole_coarse = lax.all_gather(row_total, 'row', axis=0, tiled=True)]
    ppermute x4, waiting for transfers between devices: 9.19 us -> 4.97 us  [extended(): lax.ppermute(tail, axis, [(i, (i + 1) % count) for i in range(ends)])]
  transfers between devices with their start and end apart: 9 -> 8, of which waited for: 7 -> 6; matrix products, arithmetic and copies ran while one was open for 0% -> 0% of each run, Pallas kernels for 0% -> 0%
where the time goes in v1:
time: 164 us; the launch traced here: 163 us
  blocking collectives  112 us (68%)
  starting transfers between devices  18.9 us (12%)
  waiting for transfers between devices  13.5 us (8%)
  other arithmetic  12.6 us (8%)
  local copies, waits for them, and re-layouts  2.82 us (2%)
  matrix products  2.55 us (2%)
    all_gather x1, blocking collectives, shards(): lax.all_gather(a, ('row', 'col'), axis=0, tiled=True)  68.6 us
    all_gather x1, blocking collectives, shards(): row_total = jnp.sum(lax.all_gather(product, 'col'), axis=0)  31.6 us
    ppermute x4, starting transfers between devices, extended(): lax.ppermute(tail, axis, [(i, (i + 1) % count) for i in range(ends)])  13.8 us
    all_gather x1, blocking collectives, shards(): whole_coarse = lax.all_gather(row_total, 'row', axis=0, tiled=True)  11.7 us
    scatter-add x1, other arithmetic, add_piece(): return carry.at[target].add(piece, mode='drop')  11.5 us
    ppermute x4, waiting for transfers between devices, extended(): lax.ppermute(head, axis, [((i + 1) % count, i) for i in range(ends)])  8.5 us
    ppermute x4, starting transfers between devices, extended(): lax.ppermute(head, axis, [((i + 1) % count, i) for i in range(ends)])  5.17 us
    ppermute x4, waiting for transfers between devices, extended(): lax.ppermute(tail, axis, [(i, (i + 1) % count) for i in range(ends)])  4.97 us
  transfers between devices with their start and end apart: 8, of which 6 were waited for; matrix products, arithmetic and copies ran while one was open for 0% of the time, Pallas kernels for 0%

profile of v1, /device:TPU:0, one launch (start us, length us, event | category | flops | bytes accessed | tf_op | source)
XLA Modules:
  0.0 162.6 jit_solution(902492372925517922)
XLA Ops:
  0.0 0.8 fusion.18
  0.8 0.8 copy_bitcast_fusion
  1.6 0.6 gather_fusion
  2.2 2.4 %collective-permute-start = (bf16[1,1,4,128,32]{3,4,2,1,0:T(8,128)(2,1)S(1)}, bf16[1,1,4,128,32]{3,4,2,1,0:T(8,128)(2,1)S(1)}, u32[]{:S(2)}, u32[]{:S(2)}) collective-permute-start(bf16[1,1,4,128,32]{3,4,2,1,0:T(8,128)(2,1)S(1)} %bitcast_select_fusion), channel_id=1, source_target_pairs={{0,8},{8,16},{16,24},{1,9},{9,17},{17,25},{2,10},{10,18},{18,26},{... | collective-permute-start | bytes 98312 | tf_op jit(solution)/shard_map/ppermute | solution.py:17
  4.6 1.3 collective-permute-start.1
  6.1 3.8 %collective-permute-done.1 = bf16[1,1,4,128,32]{3,4,2,1,0:T(8,128)(2,1)S(1)} collective-permute-done((bf16[1,1,4,128,32]{3,4,2,1,0:T(8,128)(2,1)S(1)}, bf16[1,1,4,128,32]{3,4,2,1,0:T(8,128)(2,1)S(1)}, u32[]{:S(2)}, u32[]{:S(2)}) %collective-permute-start.1) | collective-permute-done | bytes 32800 | tf_op jit(solution)/shard_map/ppermute | solution.py:19
  9.9 1.3 collective-permute-start.3
  11.2 4.6 %collective-permute-start.2 = (bf16[3,1,4,128,32]{3,4,2,1,0:T(8,128)(2,1)S(1)}, bf16[3,1,4,128,32]{3,4,2,1,0:T(8,128)(2,1)S(1)}, u32[]{:S(2)}, u32[]{:S(2)}) collective-permute-start(bf16[3,1,4,128,32]{3,4,2,1,0:T(8,128)(2,1)S(1)} %pad_maximum_fusion), channel_id=1, source_target_pairs={{0,1},{1,2},{2,3},{3,4},{4,5},{5,6},{6,7},{8,9},{9,10},{10,11},{11... | collective-permute-start | bytes 294920 | tf_op jit(solution)/shard_map/ppermute | solution.py:17
  15.7 0.6 collective-permute-done.3
  16.4 3.2 %collective-permute-done.2 = bf16[3,1,4,128,32]{3,4,2,1,0:T(8,128)(2,1)S(1)} collective-permute-done((bf16[3,1,4,128,32]{3,4,2,1,0:T(8,128)(2,1)S(1)}, bf16[3,1,4,128,32]{3,4,2,1,0:T(8,128)(2,1)S(1)}, u32[]{:S(2)}, u32[]{:S(2)}) %collective-permute-start.2) | collective-permute-done | bytes 98336 | tf_op jit(solution)/shard_map/ppermute | solution.py:17
  19.9 68.6 %all-gather.1 = f32[32,64,32]{1,2,0:T(8,128)S(1)} all-gather(f32[1,64,32]{1,2,0:T(8,128)S(1)} %convolution_bitcast_fusion.3), channel_id=1, replica_groups=mesh['row'=4,'col'=8] {'row','col'}, dimensions={0}, use_global_device_ids=true | all-gather | bytes 270336 | tf_op jit(solution)/shard_map/all_gather | solution.py:51
  88.8 11.5 %scatter_custom_fusion = f32[256,32]{1,0:T(8,128)S(1)} fusion(s32[2048]{0:T(1024)S(1)} %compare_select_fusion, f32[2048,32]{1,0:T(8,128)S(1)} %bitcast.74, f32[]{:T(128)} %constant.49.clone.1), kind=kCustom, calls=%fused_computation.19 | custom fusion | flops 65536 | bytes 32772 | tf_op jit(solution)/shard_map/scatter-add | solution.py:47
  100.3 0.6 convolution_bitcast_fusion.1
  101.0 31.6 %all-gather = f32[4096,32]{0,1:T(8,128)S(1)} all-gather(f32[512,32]{0,1:T(8,128)S(1)} %convolution_bitcast_fusion.1), channel_id=2, replica_groups=mesh['row'=4,'col'=8] {'col'}, dimensions={0}, use_global_device_ids=true | all-gather | bytes 589824 | tf_op jit(solution)/shard_map/all_gather | solution.py:54
  133.1 11.7 %all_gather.15 = f32[2048,32]{1,0:T(8,128)S(1)} all-gather(f32[512,32]{1,0:T(8,128)S(1)} %copy.38), channel_id=1, replica_groups=mesh['row'=4,'col'=8] {'row'}, dimensions={0}, use_global_device_ids=true | all-gather | bytes 327680 | tf_op jit(solution)/shard_map/all_gather | solution.py:55
  144.9 0.6 gather_fusion.1
  145.9 2.3 %collective-permute-start.5 = (f32[1,1,4,128,32]{3,4,2,1,0:T(8,128)S(1)}, f32[1,1,4,128,32]{3,4,2,1,0:T(8,128)S(1)}, u32[]{:S(2)}, u32[]{:S(2)}) collective-permute-start(f32[1,1,4,128,32]{3,4,2,1,0:T(8,128)S(1)} %copy.39), channel_id=1, source_target_pairs={{0,8},{8,16},{16,24},{1,9},{9,17},{17,25},{2,10},{10,18},{18,26},{... | collective-permute-start | bytes 196616 | tf_op jit(solution)/shard_map/ppermute | solution.py:17
  148.2 1.3 collective-permute-start.4
  149.5 1.8 %collective-permute-done.4 = f32[1,1,4,128,32]{3,4,2,1,0:T(8,128)S(1)} collective-permute-done((f32[1,1,4,128,32]{3,4,2,1,0:T(8,128)S(1)}, f32[1,1,4,128,32]{3,4,2,1,0:T(8,128)S(1)}, u32[]{:S(2)}, u32[]{:S(2)}) %collective-permute-start.4) | collective-permute-done | bytes 65568 | tf_op jit(solution)/shard_map/ppermute | solution.py:19
  151.4 1.3 collective-permute-start.6
  152.7 4.6 %collective-permute-start.7 = (f32[3,1,4,128,32]{3,4,2,1,0:T(8,128)S(1)}, f32[3,1,4,128,32]{3,4,2,1,0:T(8,128)S(1)}, u32[]{:S(2)}, u32[]{:S(2)}) collective-permute-start(f32[3,1,4,128,32]{3,4,2,1,0:T(8,128)S(1)} %constant_dynamic-update-slice_fusion.1), channel_id=1, source_target_pairs={{0,1},{1,2},{2,3},{3,4},{4,5},{5,6},{6,7},{8,9},{9,10},{10,11},{11... | collective-permute-start | bytes 589832 | tf_op jit(solution)/shard_map/ppermute | solution.py:17
  157.2 2.3 %collective-permute-done.6 = f32[3,1,4,128,32]{3,4,2,1,0:T(8,128)S(1)} collective-permute-done((f32[3,1,4,128,32]{3,4,2,1,0:T(8,128)S(1)}, f32[3,1,4,128,32]{3,4,2,1,0:T(8,128)S(1)}, u32[]{:S(2)}, u32[]{:S(2)}) %collective-permute-start.6) | collective-permute-done | bytes 196640 | tf_op jit(solution)/shard_map/ppermute | solution.py:19
  159.6 1.7 %collective-permute-done.7 = f32[3,1,4,128,32]{3,4,2,1,0:T(8,128)S(1)} collective-permute-done((f32[3,1,4,128,32]{3,4,2,1,0:T(8,128)S(1)}, f32[3,1,4,128,32]{3,4,2,1,0:T(8,128)S(1)}, u32[]{:S(2)}, u32[]{:S(2)}) %collective-permute-start.7) | collective-permute-done | bytes 196640 | tf_op jit(solution)/shard_map/ppermute | solution.py:17
  161.6 1.1 fusion.1
  (50 shorter events, 2.1 us)
Async XLA Ops:
  0.0 161.5 %copy-start = (bf16[512,1024]{1,0:T(8,128)(2,1)S(1)}, bf16[512,1024]{1,0:T(8,128)(2,1)}, u32[]{:S(2)}) copy-start(bf16[512,1024]{1,0:T(8,128)(2,1)} %param.8) | copy-start | bytes 3145732
  0.0 0.8 copy-start.7
  1.6 4.4 %copy-start.3 = (bf16[512,32]{0,1:T(8,128)(2,1)S(1)}, bf16[512,32]{0,1:T(8,128)(2,1)}, u32[]{:S(2)}) copy-start(bf16[512,32]{0,1:T(8,128)(2,1)} %param.6) | copy-start | bytes 98308
  1.6 4.4 %copy-start.6 = (s32[2048]{0:T(1024)S(1)}, s32[2048]{0:T(1024)}, u32[]{:S(2)}) copy-start(s32[2048]{0:T(1024)} %param.10) | copy-start | bytes 24580
  2.1 17.5 %copy-start.1 = (f32[1024,64]{0,1:T(8,128)S(1)}, f32[1024,64]{0,1:T(8,128)}, u32[]{:S(2)}) copy-start(f32[1024,64]{0,1:T(8,128)} %param.9) | copy-start | bytes 786436
  2.2 3.8 %collective-permute-start = (bf16[1,1,4,128,32]{3,4,2,1,0:T(8,128)(2,1)S(1)}, bf16[1,1,4,128,32]{3,4,2,1,0:T(8,128)(2,1)S(1)}, u32[]{:S(2)}, u32[]{:S(2)}) collective-permute-start(bf16[1,1,4,128,32]{3,4,2,1,0:T(8,128)(2,1)S(1)} %bitcast_select_fusion), channel_id=1, source_target_pairs={{0,8},{8,16},{16,24},{1,9},{9,17},{17,25},{2,10},{10,18},{18,26},{... | collective-permute-start | bytes 98312 | tf_op jit(solution)/shard_map/ppermute | solution.py:17
  4.6 5.2 %collective-permute-start.1 = (bf16[1,1,4,128,32]{3,4,2,1,0:T(8,128)(2,1)S(1)}, bf16[1,1,4,128,32]{3,4,2,1,0:T(8,128)(2,1)S(1)}, u32[]{:S(2)}, u32[]{:S(2)}) collective-permute-start(bf16[1,1,4,128,32]{3,4,2,1,0:T(8,128)(2,1)S(1)} %bitcast_select_fusion), channel_id=1, source_target_pairs={{8,0},{16,8},{24,16},{9,1},{17,9},{25,17},{10,2},{18,10},{26,18},{... | collective-permute-start | bytes 98312 | tf_op jit(solution)/shard_map/ppermute | solution.py:19
  9.9 6.5 %collective-permute-start.3 = (bf16[3,1,4,128,32]{3,4,2,1,0:T(8,128)(2,1)S(1)}, bf16[3,1,4,128,32]{3,4,2,1,0:T(8,128)(2,1)S(1)}, u32[]{:S(2)}, u32[]{:S(2)}) collective-permute-start(bf16[3,1,4,128,32]{3,4,2,1,0:T(8,128)(2,1)S(1)} %pad_maximum_fusion), channel_id=1, source_target_pairs={{1,0},{2,1},{3,2},{4,3},{5,4},{6,5},{7,6},{9,8},{10,9},{11,10},{12... | collective-permute-start | bytes 294920 | tf_op jit(solution)/shard_map/ppermute | solution.py:19
  11.2 8.4 %collective-permute-start.2 = (bf16[3,1,4,128,32]{3,4,2,1,0:T(8,128)(2,1)S(1)}, bf16[3,1,4,128,32]{3,4,2,1,0:T(8,128)(2,1)S(1)}, u32[]{:S(2)}, u32[]{:S(2)}) collective-permute-start(bf16[3,1,4,128,32]{3,4,2,1,0:T(8,128)(2,1)S(1)} %pad_maximum_fusion), channel_id=1, source_target_pairs={{0,1},{1,2},{2,3},{3,4},{4,5},{5,6},{6,7},{8,9},{9,10},{10,11},{11... | collective-permute-start | bytes 294920 | tf_op jit(solution)/shard_map/ppermute | solution.py:17
  88.5 11.9 %copy-start.2 = (f32[512,256]{1,0:T(8,128)S(1)}, f32[512,256]{1,0:T(8,128)}, u32[]{:S(2)}) copy-start(f32[512,256]{1,0:T(8,128)} %param.11) | copy-start | bytes 1572868
  145.9 3.6 %collective-permute-start.5 = (f32[1,1,4,128,32]{3,4,2,1,0:T(8,128)S(1)}, f32[1,1,4,128,32]{3,4,2,1,0:T(8,128)S(1)}, u32[]{:S(2)}, u32[]{:S(2)}) collective-permute-start(f32[1,1,4,128,32]{3,4,2,1,0:T(8,128)S(1)} %copy.39), channel_id=1, source_target_pairs={{0,8},{8,16},{16,24},{1,9},{9,17},{17,25},{2,10},{10,18},{18,26},{... | collective-permute-start | bytes 196616 | tf_op jit(solution)/shard_map/ppermute | solution.py:17
  148.2 3.1 %collective-permute-start.4 = (f32[1,1,4,128,32]{3,4,2,1,0:T(8,128)S(1)}, f32[1,1,4,128,32]{3,4,2,1,0:T(8,128)S(1)}, u32[]{:S(2)}, u32[]{:S(2)}) collective-permute-start(f32[1,1,4,128,32]{3,4,2,1,0:T(8,128)S(1)} %copy.39), channel_id=1, source_target_pairs={{8,0},{16,8},{24,16},{9,1},{17,9},{25,17},{10,2},{18,10},{26,18},{... | collective-permute-start | bytes 196616 | tf_op jit(solution)/shard_map/ppermute | solution.py:19
  149.5 7.7 %copy-start.4 = (f32[1,1,4,128,32]{3,4,2,1,0:T(8,128)}, f32[1,1,4,128,32]{3,4,2,1,0:T(8,128)S(1)}, u32[]{:S(2)}) copy-start(f32[1,1,4,128,32]{3,4,2,1,0:T(8,128)S(1)} %collective-permute-done.5) | copy-start | bytes 196612
  151.3 5.9 %copy-start.5 = (f32[1,1,4,128,32]{3,4,2,1,0:T(8,128)}, f32[1,1,4,128,32]{3,4,2,1,0:T(8,128)S(1)}, u32[]{:S(2)}) copy-start(f32[1,1,4,128,32]{3,4,2,1,0:T(8,128)S(1)} %collective-permute-done.4) | copy-start | bytes 196612
  151.4 8.2 %collective-permute-start.6 = (f32[3,1,4,128,32]{3,4,2,1,0:T(8,128)S(1)}, f32[3,1,4,128,32]{3,4,2,1,0:T(8,128)S(1)}, u32[]{:S(2)}, u32[]{:S(2)}) collective-permute-start(f32[3,1,4,128,32]{3,4,2,1,0:T(8,128)S(1)} %constant_dynamic-update-slice_fusion.1), channel_id=1, source_target_pairs={{1,0},{2,1},{3,2},{4,3},{5,4},{6,5},{7,6},{9,8},{10,9},{11,10},{12... | collective-permute-start | bytes 589832 | tf_op jit(solution)/shard_map/ppermute | solution.py:19
  152.7 8.6 %collective-permute-start.7 = (f32[3,1,4,128,32]{3,4,2,1,0:T(8,128)S(1)}, f32[3,1,4,128,32]{3,4,2,1,0:T(8,128)S(1)}, u32[]{:S(2)}, u32[]{:S(2)}) collective-permute-start(f32[3,1,4,128,32]{3,4,2,1,0:T(8,128)S(1)} %constant_dynamic-update-slice_fusion.1), channel_id=1, source_target_pairs={{0,1},{1,2},{2,3},{3,4},{4,5},{5,6},{6,7},{8,9},{9,10},{10,11},{11... | collective-permute-start | bytes 589832 | tf_op jit(solution)/shard_map/ppermute | solution.py:17
  159.5 1.7 %slice-start = ((f32[1,1,4,128,32]{3,4,2,1,0:T(8,128)}), f32[1,1,1,128,32]{3,4,2,1,0:T(8,128)S(1)}, s32[]{:S(2)}) async-start(f32[1,1,4,128,32]{3,4,2,1,0:T(8,128)} %copy-done.4), calls=%async_computation | async-start | bytes 32768 | tf_op jit(solution)/shard_map/slice | solution.py:64
  159.6 1.7 %slice-start.1 = ((f32[1,1,4,128,32]{3,4,2,1,0:T(8,128)}), f32[1,1,1,128,32]{3,4,2,1,0:T(8,128)S(1)}, s32[]{:S(2)}) async-start(f32[1,1,4,128,32]{3,4,2,1,0:T(8,128)} %copy-done.5), calls=%async_computation.1 | async-start | bytes 32768 | tf_op jit(solution)/shard_map/slice | solution.py:64
